TPU v7x, 16 devices: a 4x2x1 block of a 4x4x8 slice. The times are simulated.
16 devices in a mesh: data: 2 (over y, z), tp: 8 (over x, core).
Axes of the slice: x: 4, y: 2, z: 1, core: 2. Of those that a mesh axis runs over, the one named last changes fastest.
The devices are a block of a 4x4x8 slice.
Arguments:
- attn_out: bfloat16 [1024, 12288], P('data', 'tp'), parts along dimension 0
- w_out: bfloat16 [12288, 12288], P('tp')
- residual: bfloat16 [1024, 12288], P('data', 'tp'), parts along dimension 0
- norm_gain: float32 [12288], P('tp')
Outputs:
- output 1: bfloat16 [1024, 12288], P('data', 'tp'), parts along dimension 0
- output 2: bfloat16 [1024, 12288], P('data', 'tp'), parts along dimension 0
There are 2 independent parts. A program takes and returns all parts, laid end to end along the dimension named above; an argument that names none is the same for every part.
All inputs are finite; a program needn't handle non-finite values.
Results may differ from a plain program's by a relative error of at most 0.00634263.
Values are sent between devices in bfloat16 or wider.
A program may use at most 768 MiB of HBM per device.

v0:
```python
import functools

import jax
import jax.numpy as jnp
from jax import lax
from jax.experimental import pallas as pl
from jax.experimental.pallas import tpu as pltpu
from jax.sharding import PartitionSpec as P

EPS = 1e-5
MESH = pl.DeviceIdType.MESH
CORES = 2
CHIPS = 4
UNIT = 256
W_SLOTS = 4
RB = 64
RELAY_ROWS = (256, 192, 64)
LANES = 128
FIRST_ROWS = (128, 384)


def sum_rows():
    return -(-sum(RELAY_ROWS[:-1]) // LANES), -(-RELAY_ROWS[-1] // LANES)


def _kernel(
    tp_size, d_model,
    a_hbm, w_hbm, r_hbm, g_hbm, hid, nrm,
    a, w, p, rx, relay_out, relay_in, res, gain, hbuf, sq_out, sq_in,
    a_sem, w_sem, send_sem, recv_sem, rrecv_sem, qsend_sem, qrecv_sem,
):
    rows, d_local = r_hbm.shape
    half = d_local // 2
    nu = half // UNIT
    per_group = CORES * 2 * nu
    total = CHIPS * per_group
    chunks = rows // RB

    me = lax.axis_index("tp")
    x, c = lax.div(me, CORES), lax.rem(me, CORES)

    at_first, at_last = lax.div(CHIPS - x, CHIPS), lax.div(x, CHIPS - 1)
    flip = at_first + at_last

    def chip(offset, core):
        return lax.rem(x + offset, CHIPS) * CORES + core

    def decode(s):
        g, j = lax.div(s, per_group), lax.rem(s, per_group)
        late = lax.div(lax.div(s, 2 * nu) + 7, 8)
        more = lax.div(lax.div(s, 2) + 1, 2)
        b = late * lax.div(j, nu) + (1 - late) * ((1 - more) * s + more * (lax.div(s, 2) - 1))
        i = late * lax.rem(j, nu) + (1 - late) * more * (1 + lax.rem(s, 2))
        return g, i, b, lax.rem(lax.div(b, 2) + 1 + c, 2), lax.rem(b + c + flip, 2)

    def w_copy(s):
        g, i, _, e, h = decode(s)
        o = lax.rem(6 - g + 2 * h * lax.rem(g, 2), CHIPS)
        col = pl.multiple_of(chip(o, e) * d_local + h * half + i * UNIT, UNIT)
        k = lax.rem(s, W_SLOTS)
        return pltpu.make_async_copy(w_hbm.at[:, pl.ds(col, UNIT)], w.at[k], w_sem.at[k])

    first_lo = [sum(FIRST_ROWS[:b]) for b in range(len(FIRST_ROWS))]

    def a_copy(b):
        rs = pl.ds(first_lo[b], FIRST_ROWS[b])
        return pltpu.make_async_copy(a_hbm.at[rs, :], a.at[rs, :], a_sem.at[b])

    def send(src, dst, group, target):
        pltpu.make_async_remote_copy(
            src_ref=src, dst_ref=dst, send_sem=send_sem.at[0], recv_sem=recv_sem.at[group],
            device_id={"tp": target}, device_id_type=MESH).start()

    def send_units(g, b, lo, n, block, group, target):
        send(p.at[pl.ds((g * 4 + b) * nu + lo, n)], rx.at[pl.ds(block * nu + lo, n)], group, target)

    def wait_bytes(ref, sem):
        pltpu.make_async_copy(ref, ref, sem).wait()

    def local_unit(g, h, i):
        return (g * 4 + (2 if g == 2 else 0) + lax.rem(h + c + flip, 2)) * nu + i

    relay_lo = [sum(RELAY_ROWS[:m]) for m in range(len(RELAY_ROWS))]

    def relay_rows(m):
        return pl.ds(relay_lo[m], RELAY_ROWS[m])

    def send_relay(m):
        for h in range(2):
            pltpu.make_async_remote_copy(
                src_ref=relay_out.at[h, relay_rows(m)], dst_ref=relay_in.at[h, relay_rows(m)],
                send_sem=send_sem.at[0], recv_sem=rrecv_sem.at[m],
                device_id={"tp": chip(3 - 2 * h, 1 - c)}, device_id_type=MESH).start()

    def chunk_rows(r):
        return pl.ds(pl.multiple_of(r * RB, RB), RB)

    def span(lo, n):
        return pl.ds(pl.multiple_of(lo, n), n)

    w_copy(jnp.int32(0)).start()
    a_copy(0).start()
    w_copy(jnp.int32(1)).start()

    peers = [x * CORES + 1 - c] + [chip(o, core) for o in (1, CHIPS - 1) for core in range(CORES)]
    barrier = pltpu.get_barrier_semaphore()
    for peer in peers:
        pl.semaphore_signal(barrier, inc=1, device_id={"tp": peer}, device_id_type=MESH)

    for b in range(1, len(FIRST_ROWS)):
        a_copy(b).start()
    r_copy = pltpu.make_async_copy(r_hbm, res, a_sem.at[0])
    g_copy = pltpu.make_async_copy(g_hbm, gain, a_sem.at[1])

    for b in range(len(FIRST_ROWS)):
        rs = pl.ds(first_lo[b], FIRST_ROWS[b])
        for s in range(2):
            _, _, block, e0, h0 = decode(jnp.int32(s))
            if b == 0:
                with jax.named_scope(f"w{s}"):
                    w_copy(jnp.int32(s)).wait()
            if s == 0:
                with jax.named_scope("awt"):
                    a_copy(b).wait()
            if b == 0 and s == 0:
                for k in range(2, W_SLOTS):
                    w_copy(jnp.int32(k)).start()
            unit = block * nu
            p[unit, rs, :] = jnp.dot(a[rs, :], w[s], preferred_element_type=jnp.float32).astype(p.dtype)
            if b == 0 and s == 0:
                with jax.named_scope("bar"):
                    pl.semaphore_wait(barrier, len(peers))
            send(p.at[unit, rs], rx.at[(h0 * 2 + c) * nu, rs], 0, chip(3 + 2 * h0, 1 - e0))
    for s in range(2):
        w_copy(jnp.int32(s + W_SLOTS)).start()
    r_copy.start()
    g_copy.start()

    @pl.loop(2, total)
    def _(s):
        g, i, b, e, h = decode(s)
        w_copy(s).wait()
        k = lax.rem(s, W_SLOTS)
        p[(g * 4 + b) * nu + i] = jnp.dot(
            a[...], w[k], preferred_element_type=jnp.float32).astype(p.dtype)

        @pl.when(s + W_SLOTS < total)
        def _():
            w_copy(s + W_SLOTS).start()

        def to_relay(lo, n):
            send_units(g, b, lo, n, h * 2 + c, 0, chip(3 + 2 * h, 1 - e))

        @pl.when(i == nu - 1)
        def _():
            @pl.when(s < 2 * nu)
            def _():
                to_relay(1, nu - 1)

            @pl.when(jnp.logical_and(g == 0, s >= 2 * nu))
            def _():
                to_relay(0, nu)

            @pl.when(g == 1)
            def _():
                send_units(g, b, 0, nu, 4 + h * 2 + c, 1, chip(1 + 2 * h, e))

            @pl.when(jnp.logical_or(jnp.logical_and(g == 2, b < 2), jnp.logical_and(g == 3, b >= 2)))
            def _():
                send_units(g, b, 0, nu, 4 + g * 2 + h, 3 - g, x * CORES + 1 - c)

    with jax.named_scope("l2r"):
        wait_bytes(rx.at[pl.ds(0, 6 * nu)], recv_sem.at[0])

    @pl.loop(0, chunks)
    def _(r):
        rs = chunk_rows(r)
        for h in range(2):
            for i in range(nu):
                acc = p[local_unit(3, h, i), rs, :].astype(jnp.float32)
                acc += rx[(10 + h) * nu + i, rs, :].astype(jnp.float32)
                acc += rx[(h * 2) * nu + i, rs, :].astype(jnp.float32)
                acc += rx[(h * 2 + 1) * nu + i, rs, :].astype(jnp.float32)
                relay_out[h, rs, i * UNIT:(i + 1) * UNIT] = acc

    for m in range(len(RELAY_ROWS)):
        send_relay(m)

    r_copy.wait()
    g_copy.wait()
    with jax.named_scope("direct"):
        wait_bytes(rx.at[pl.ds(0, 6 * nu)], recv_sem.at[1])

    sq_n = sum_rows()
    sq_lo = (0, sq_n[0])

    def on_lane(lane, n):
        return (lax.broadcasted_iota(jnp.int32, (n, LANES), 0) + lane
                == lax.broadcasted_iota(jnp.int32, (n, LANES), 1))

    def columns():
        for h in range(2):
            for i in range(nu):
                yield h, i, slice(h * half + i * UNIT, h * half + (i + 1) * UNIT)

    def add_early(lo, n):
        rs = span(lo, n)
        for h, i, cols in columns():
            acc = p[local_unit(2, h, i), rs, :].astype(jnp.float32)
            acc += rx[(8 + h) * nu + i, rs, :].astype(jnp.float32)
            acc += rx[(4 + h * 2) * nu + i, rs, :].astype(jnp.float32)
            acc += rx[(5 + h * 2) * nu + i, rs, :].astype(jnp.float32)
            hbuf[rs, cols] = acc + res[rs, cols].astype(jnp.float32)

    def finish(m, lo, n):
        rs = span(lo, n)
        sq = jnp.zeros((n, UNIT), jnp.float32)
        for h, i, cols in columns():
            acc = hbuf[rs, cols] + relay_in[h, rs, i * UNIT:(i + 1) * UNIT]
            hbuf[rs, cols] = acc
            sq += acc * acc
        sq = jnp.sum(sq, axis=1, keepdims=True)
        q, lane = place(m, lo)
        sq_out[q] += jnp.sum(
            jnp.where(on_lane(lane, n), jnp.broadcast_to(sq, (n, LANES)), 0.0), axis=0, keepdims=True)

    def place(m, lo):
        if m == len(RELAY_ROWS) - 1:
            lo = lo - relay_lo[m]
            return sq_lo[1] + lax.div(lo, LANES), lax.rem(lo, LANES)
        return lax.div(lo, LANES), lax.rem(lo, LANES)

    first = 3 * at_first + at_last + 2 * (1 - flip)
    second = 1 + flip
    others = [chip(o, core) for o in (first, second, 6 - first - second) for core in range(CORES)]
    others.append(x * CORES + 1 - c)

    def send_sums(k):
        for target in others:
            pltpu.make_async_remote_copy(
                src_ref=sq_out.at[sq_span(k)], dst_ref=sq_in.at[me, sq_span(k)],
                send_sem=qsend_sem.at[0], recv_sem=qrecv_sem.at[k],
                device_id={"tp": target}, device_id_type=MESH).start()
        for q in range(sq_lo[k], sq_lo[k] + sq_n[k]):
            sq_in[me, q] = sq_out[q]

    def sq_span(k):
        return pl.ds(sq_lo[k], sq_n[k])

    def wait_sums(k, sem):
        wait_bytes(sq_in.at[pl.ds(0, tp_size - 1), sq_span(k)], sem.at[k])

    def normalise(m, lo, n):
        q, lane = place(m, lo)
        tot = sq_in[0, q]
        for t in range(1, tp_size):
            tot += sq_in[t, q]
        col = jnp.sum(jnp.where(on_lane(lane, n), jnp.broadcast_to(tot, (n, LANES)), 0.0), axis=1, keepdims=True)
        scale = lax.rsqrt(col / d_model + EPS)
        rs = span(lo, n)
        nrm[rs, :] = (hbuf[rs, :] * scale * gain[...].reshape(1, d_local)).astype(nrm.dtype)

    def write_hidden(lo, n):
        rs = span(lo, n)
        hid[rs, :] = hbuf[rs, :].astype(hid.dtype)

    def each(m, *steps):
        lo, hi = relay_lo[m], relay_lo[m] + RELAY_ROWS[m]
        whole = (hi - lo) // RB * RB

        if whole:
            @pl.loop(0, whole // RB)
            def _(r):
                for step in steps:
                    step(lo + r * RB, RB)

        if lo + whole < hi:
            for step in steps:
                step(lo + whole, hi - lo - whole)

    def wait_relay(m):
        with jax.named_scope(f"r{m}"):
            wait_bytes(relay_in.at[:, relay_rows(m)], rrecv_sem.at[m])

    for q in range(sum(sq_n)):
        sq_out[q] = jnp.zeros((1, LANES), jnp.float32)
    last = len(RELAY_ROWS) - 1
    for m in range(last + 1):
        each(m, add_early)
        wait_relay(m)
        each(m, functools.partial(finish, m))
        if m >= last - 1:
            send_sums(m - last + 1)
        each(m, write_hidden)

    wait_bytes(p, send_sem.at[0])
    for m in range(last + 1):
        if m in (0, last):
            with jax.named_scope(f"sq{m}"):
                wait_sums(min(m, 1), qrecv_sem)
        each(m, functools.partial(normalise, m))
    with jax.named_scope("qdrain"):
        wait_bytes(sq_in.at[pl.ds(0, tp_size - 1)], qsend_sem.at[0])


def _write(hid, nrm, hid_hbm, nrm_hbm, sem):
    blocks = 4
    rows = hid.shape[0] // blocks
    pairs = ((hid, hid_hbm), (nrm, nrm_hbm))
    for k, (src, dst) in enumerate(pairs):
        for b in range(blocks):
            rs = pl.ds(b * rows, rows)
            pltpu.make_async_copy(src.at[rs, :], dst.at[rs, :], sem.at[k]).start()
    for k, (src, dst) in enumerate(pairs):
        pltpu.make_async_copy(src, dst, sem.at[k]).wait()


def solution(mesh):
    tp_size = mesh.shape["tp"]

    def local_step(attn_blk, w_blk, resid_blk, gain_blk):
        rows, k_dim = attn_blk.shape
        d_local = resid_blk.shape[1]
        d_model = w_blk.shape[1]
        half = d_local // 2
        nu = half // UNIT
        units = tp_size * 2 * nu
        sq_rows = sum(sum_rows())
        assert tp_size == CORES * CHIPS and half % UNIT == 0
        assert sum(FIRST_ROWS) == sum(RELAY_ROWS) == rows and rows % RB == 0 and nu == 3
        hbm_spec = pl.BlockSpec(memory_space=pltpu.HBM)
        vmem_spec = pl.BlockSpec(memory_space=pltpu.VMEM)
        dma = pltpu.SemaphoreType.DMA
        out_shape = [jax.ShapeDtypeStruct((rows, d_local), jnp.bfloat16)] * 2
        hid, nrm = pl.pallas_call(
            functools.partial(_kernel, tp_size, d_model),
            out_shape=[pltpu.VMEM((rows, d_local), jnp.bfloat16)] * 2,
            in_specs=[hbm_spec] * 4,
            out_specs=[vmem_spec] * 2,
            scratch_shapes=[
                pltpu.VMEM((rows, k_dim), jnp.bfloat16),
                pltpu.VMEM((W_SLOTS, k_dim, UNIT), jnp.bfloat16),
                pltpu.VMEM((units, rows, UNIT), jnp.bfloat16),
                pltpu.VMEM((12 * nu, rows, UNIT), jnp.bfloat16),
                pltpu.VMEM((2, rows, half), jnp.float32),
                pltpu.VMEM((2, rows, half), jnp.float32),
                pltpu.VMEM((rows, d_local), jnp.bfloat16),
                pltpu.VMEM((d_local,), jnp.float32),
                pltpu.VMEM((rows, d_local), jnp.float32),
                pltpu.VMEM((sq_rows, 1, LANES), jnp.float32),
                pltpu.VMEM((tp_size, sq_rows, 1, LANES), jnp.float32),
                dma((len(FIRST_ROWS),)),
                dma((W_SLOTS,)),
                dma((1,)),
                dma((2,)),
                dma((len(RELAY_ROWS),)),
                dma((1,)),
                dma((2,)),
            ],
            compiler_params=pltpu.CompilerParams(
                collective_id=0, has_side_effects=True, vmem_limit_bytes=62 * 1000 * 1000
            ),
            name="proj_scatter_norm",
        )(attn_blk, w_blk, resid_blk, gain_blk)
        return pl.pallas_call(
            _write,
            out_shape=out_shape,
            in_specs=[vmem_spec] * 2,
            out_specs=[hbm_spec] * 2,
            scratch_shapes=[dma((2,))],
            compiler_params=pltpu.CompilerParams(vmem_limit_bytes=8 * 1024 * 1024),
            name="write_out",
        )(hid, nrm)

    return jax.shard_map(
        local_step,
        mesh=mesh,
        in_specs=(P("data", "tp"), P("tp", None), P("data", "tp"), P("tp")),
        out_specs=(P("data", "tp"), P("data", "tp")),
        check_vma=False,
    )
```

profile of v0, /device:TPU:113, one launch (start us, length us, event | category | flops | bytes accessed | tf_op | source)
XLA Modules:
  0.0 113.1 jit_solution(12934153957029874717)
XLA Ops:
  0.6 110.8 %proj_scatter_norm.1 = (bf16[512,1536]{1,0:T(8,128)(2,1)S(1)}, bf16[512,1536]{1,0:T(8,128)(2,1)S(1)}) custom-call(bf16[512,1536]{1,0:T(8,128)(2,1)} %a_hbm.1, bf16[1536,12288]{1,0:T(8,128)(2,1)} %w_hbm.1, bf16[512,1536]{1,0:T(8,128)(2,1)} %r_hbm.1, f32[1536]{0:T(1024)} %g_hbm.1), custom_call_target="tpu_custom_call" | custom-call | tf_op jit(solution)/shard_map/proj_scatter_norm/pallas_call | solution.py:335
  111.4 1.7 %write_out.1 = (bf16[512,1536]{1,0:T(8,128)(2,1)}, bf16[512,1536]{1,0:T(8,128)(2,1)}) custom-call(bf16[512,1536]{1,0:T(8,128)(2,1)S(1)} %get-tuple-element.4.hid, bf16[512,1536]{1,0:T(8,128)(2,1)S(1)} %get-tuple-element.5.nrm), custom_call_target="tpu_custom_call" | custom-call | tf_op jit(solution)/shard_map/write_out/pallas_call | solution.py:365
where the time goes:
time: 113 us
  Pallas kernels  112 us (99%)
    pallas_call x1, Pallas kernels, local_step(): pl.pallas_call(functools.partial(_kernel, tp_size, d_model), out_shape=[p...  111 us

commit v1 on v0

--- a/solution.py
+++ b/solution.py
@@ -14,13 +14,14 @@
 UNIT = 256
 W_SLOTS = 4
 RB = 64
-RELAY_ROWS = (256, 192, 64)
+RELAY_ROWS = (256, 192, 32, 32)
+EARLY = 2
 LANES = 128
 FIRST_ROWS = (128, 384)
 
 
 def sum_rows():
-    return -(-sum(RELAY_ROWS[:-1]) // LANES), -(-RELAY_ROWS[-1] // LANES)
+    return -(-sum(RELAY_ROWS[:EARLY]) // LANES), -(-sum(RELAY_ROWS[EARLY:]) // LANES)
 
 
 def _kernel(
@@ -225,8 +226,8 @@
             jnp.where(on_lane(lane, n), jnp.broadcast_to(sq, (n, LANES)), 0.0), axis=0, keepdims=True)
 
     def place(m, lo):
-        if m == len(RELAY_ROWS) - 1:
-            lo = lo - relay_lo[m]
+        if m >= EARLY:
+            lo = lo - relay_lo[EARLY]
             return sq_lo[1] + lax.div(lo, LANES), lax.rem(lo, LANES)
         return lax.div(lo, LANES), lax.rem(lo, LANES)
 
@@ -289,15 +290,15 @@
         each(m, add_early)
         wait_relay(m)
         each(m, functools.partial(finish, m))
-        if m >= last - 1:
-            send_sums(m - last + 1)
+        if m in (EARLY - 1, last):
+            send_sums(int(m == last))
         each(m, write_hidden)
 
     wait_bytes(p, send_sem.at[0])
     for m in range(last + 1):
-        if m in (0, last):
+        if m in (0, EARLY):
             with jax.named_scope(f"sq{m}"):
-                wait_sums(min(m, 1), qrecv_sem)
+                wait_sums(m // EARLY, qrecv_sem)
         each(m, functools.partial(normalise, m))
     with jax.named_scope("qdrain"):
         wait_bytes(sq_in.at[pl.ds(0, tp_size - 1)], qsend_sem.at[0])

time: 113 us -> 113 us (level)
  no operation moved by 1% of the time
where the time goes in v1:
time: 113 us
  Pallas kernels  112 us (99%)
    pallas_call x1, Pallas kernels, local_step(): pl.pallas_call(functools.partial(_kernel, tp_size, d_model), out_shape=[p...  111 us

profile of v1, /device:TPU:113, one launch (start us, length us, event | category | flops | bytes accessed | tf_op | source)
XLA Modules:
  0.0 113.0 jit_solution(13358595375720362514)
XLA Ops:
  0.6 110.7 %proj_scatter_norm.1 = (bf16[512,1536]{1,0:T(8,128)(2,1)S(1)}, bf16[512,1536]{1,0:T(8,128)(2,1)S(1)}) custom-call(bf16[512,1536]{1,0:T(8,128)(2,1)} %a_hbm.1, bf16[1536,12288]{1,0:T(8,128)(2,1)} %w_hbm.1, bf16[512,1536]{1,0:T(8,128)(2,1)} %r_hbm.1, f32[1536]{0:T(1024)} %g_hbm.1), custom_call_target="tpu_custom_call" | custom-call | tf_op jit(solution)/shard_map/proj_scatter_norm/pallas_call | solution.py:336
  111.4 1.7 %write_out.1 = (bf16[512,1536]{1,0:T(8,128)(2,1)}, bf16[512,1536]{1,0:T(8,128)(2,1)}) custom-call(bf16[512,1536]{1,0:T(8,128)(2,1)S(1)} %get-tuple-element.4.hid, bf16[512,1536]{1,0:T(8,128)(2,1)S(1)} %get-tuple-element.5.nrm), custom_call_target="tpu_custom_call" | custom-call | tf_op jit(solution)/shard_map/write_out/pallas_call | solution.py:366

commit v2 on v1

--- a/solution.py
+++ b/solution.py
@@ -17,7 +17,7 @@
 RELAY_ROWS = (256, 192, 32, 32)
 EARLY = 2
 LANES = 128
-FIRST_ROWS = (128, 384)
+FIRST_ROWS = (64, 448)
 
 
 def sum_rows():

time: 113 us -> 114 us (level)
  no operation moved by 1% of the time
where the time goes in v2:
time: 114 us
  Pallas kernels  113 us (99%)
    pallas_call x1, Pallas kernels, local_step(): pl.pallas_call(functools.partial(_kernel, tp_size, d_model), out_shape=[p...  111 us

profile of v2, /device:TPU:113, one launch (start us, length us, event | category | flops | bytes accessed | tf_op | source)
XLA Modules:
  0.0 113.6 jit_solution(13115393274575108984)
XLA Ops:
  0.6 111.3 %proj_scatter_norm.1 = (bf16[512,1536]{1,0:T(8,128)(2,1)S(1)}, bf16[512,1536]{1,0:T(8,128)(2,1)S(1)}) custom-call(bf16[512,1536]{1,0:T(8,128)(2,1)} %a_hbm.1, bf16[1536,12288]{1,0:T(8,128)(2,1)} %w_hbm.1, bf16[512,1536]{1,0:T(8,128)(2,1)} %r_hbm.1, f32[1536]{0:T(1024)} %g_hbm.1), custom_call_target="tpu_custom_call" | custom-call | tf_op jit(solution)/shard_map/proj_scatter_norm/pallas_call | solution.py:336
  111.9 1.7 %write_out.1 = (bf16[512,1536]{1,0:T(8,128)(2,1)}, bf16[512,1536]{1,0:T(8,128)(2,1)}) custom-call(bf16[512,1536]{1,0:T(8,128)(2,1)S(1)} %get-tuple-element.4.hid, bf16[512,1536]{1,0:T(8,128)(2,1)S(1)} %get-tuple-element.5.nrm), custom_call_target="tpu_custom_call" | custom-call | tf_op jit(solution)/shard_map/write_out/pallas_call | solution.py:366

commit v3 on v2

--- a/solution.py
+++ b/solution.py
@@ -17,7 +17,7 @@
 RELAY_ROWS = (256, 192, 32, 32)
 EARLY = 2
 LANES = 128
-FIRST_ROWS = (64, 448)
+FIRST_ROWS = (192, 320)
 
 
 def sum_rows():

time: 114 us -> 113 us (level)
  no operation moved by 1% of the time
where the time goes in v3:
time: 113 us
  Pallas kernels  112 us (99%)
    pallas_call x1, Pallas kernels, local_step(): pl.pallas_call(functools.partial(_kernel, tp_size, d_model), out_shape=[p...  111 us

profile of v3, /device:TPU:113, one launch (start us, length us, event | category | flops | bytes accessed | tf_op | source)
XLA Modules:
  0.0 113.1 jit_solution(11988437614470775945)
XLA Ops:
  0.6 110.8 %proj_scatter_norm.1 = (bf16[512,1536]{1,0:T(8,128)(2,1)S(1)}, bf16[512,1536]{1,0:T(8,128)(2,1)S(1)}) custom-call(bf16[512,1536]{1,0:T(8,128)(2,1)} %a_hbm.1, bf16[1536,12288]{1,0:T(8,128)(2,1)} %w_hbm.1, bf16[512,1536]{1,0:T(8,128)(2,1)} %r_hbm.1, f32[1536]{0:T(1024)} %g_hbm.1), custom_call_target="tpu_custom_call" | custom-call | tf_op jit(solution)/shard_map/proj_scatter_norm/pallas_call | solution.py:336
  111.4 1.7 %write_out.1 = (bf16[512,1536]{1,0:T(8,128)(2,1)}, bf16[512,1536]{1,0:T(8,128)(2,1)}) custom-call(bf16[512,1536]{1,0:T(8,128)(2,1)S(1)} %get-tuple-element.4.hid, bf16[512,1536]{1,0:T(8,128)(2,1)S(1)} %get-tuple-element.5.nrm), custom_call_target="tpu_custom_call" | custom-call | tf_op jit(solution)/shard_map/write_out/pallas_call | solution.py:366
